TPU v7x, 32 devices: a whole 2x2x4 slice. The times are simulated.
32 devices in a mesh: parts: 2 (over y), brick: 4 (over z), rep: 2 (over x), sub: 2 (over core).
Axes of the slice: x: 2, y: 2, z: 4, core: 2. Of those that a mesh axis runs over, the one named last changes fastest.
Arguments:
- fine_cells: int32 [5, 32768], P(None, ('parts', 'brick', 'rep', 'sub')), parts along dimension 1, may hold values from 0 to 511, as said below
- fine_exponent: float32 [32768], P(('parts', 'brick', 'rep', 'sub')), parts along dimension 0, may hold values from 0.05 to 0.6
- fine_charge: float32 [32768], P(('parts', 'brick', 'rep', 'sub')), parts along dimension 0, may hold values from -6 to 6
- fine_offset: float32 [3, 32768], P(None, ('parts', 'brick', 'rep', 'sub')), parts along dimension 1, may hold values from 0 to 1
- wide_cells: int32 [5, 4096], P(None, ('parts', 'brick', 'rep', 'sub')), parts along dimension 1, may hold values from 0 to 127, as said below
- wide_exponent: float32 [4096], P(('parts', 'brick', 'rep', 'sub')), parts along dimension 0, may hold values from 0.05 to 0.6
- wide_charge: float32 [4096], P(('parts', 'brick', 'rep', 'sub')), parts along dimension 0, may hold values from -6 to 6
- wide_offset: float32 [3, 4096], P(None, ('parts', 'brick', 'rep', 'sub')), parts along dimension 1, may hold values from 0 to 1
Outputs:
- finest_grid: float32 [256, 512, 512], P(('parts', 'brick'), ('rep', 'sub')), parts along dimension 0
- second_grid: float32 [128, 256, 256], P(('parts', 'brick'), ('rep', 'sub')), parts along dimension 0
- middle_grid: float32 [64, 16384], P('parts', 'brick'), parts along dimension 0
- coarse_grid: float32 [32, 4096], P('parts', 'brick'), parts along dimension 0
- coarsest_grid: float32 [16, 1024], P('parts', 'brick'), parts along dimension 0
There are 2 independent parts, one for each index of `parts`. A program takes and returns all parts, laid end to end along the dimension named above; each array names one. Nothing has to cross between parts.
Inputs may be any that keep to these rules, and one draw needn't show every extreme that they name: `fine_cells`: column n is one fine Gaussian: row 0 its level L (0 or 1), row 1 its radius (1 to 4, equal to 4 on every 16th column), rows 2 to 4 its centre cell on level L's grid. The centre lies in the block of the device that holds column n: along the first dimension within that device's brick block of 128/2^L/4 cells, along the second within its block of 512/2^L/4 cells along rep+sub, anywhere along the third. `wide_cells`: column n is one wide Gaussian: row 0 its level L (2 to 4), row 1 its radius (1 to 4, equal to 4 on every 16th column), rows 2 to 4 its centre cell, anywhere on level L's grid.
All inputs are finite; a program needn't handle non-finite values.
Results may differ from a plain program's by a relative error of at most 0.0038.
Values sent between devices are 32-bit elements; how exact they have to be, the bound alone decides.
A program may use at most 64 MiB of HBM per device.

v0:
```python
import functools

import jax
import jax.numpy as jnp
from jax import lax
from jax.experimental import pallas as pl
from jax.experimental.pallas import tpu as pltpu
from jax.sharding import PartitionSpec as P

GRID = 512
ROWS = 128
HALF = 4
SPILL = 384
WIDE_BLOCK = 256
DIRECTIONS = [(i, j) for i in (-1, 0, 1) for j in (-1, 0, 1) if (i, j) != (0, 0)]
MESH = pl.DeviceIdType.MESH
F32 = jnp.float32
BF16 = jnp.bfloat16
I32 = jnp.int32


def exchange_kernel(bricks, reps, subs, *refs):
    fine_in, wide_in = refs[0:4], refs[4:8]
    fine_out, wide_out = refs[8:12], refs[12:16]
    fine_send, fine_recv, wide_send, wide_recv, own_sem = refs[16:]
    columns = reps * subs
    devices = bricks * columns
    brick = lax.axis_index("brick")
    column = lax.axis_index("rep") * subs + lax.axis_index("sub")
    me = brick * columns + column
    slots = fine_in[0].shape[1]
    wide_slots = wide_in[0].shape[1]

    def place(brick_at, column_at):
        return {"brick": brick_at, "rep": column_at // subs, "sub": column_at % subs}

    def other(step):
        at = lax.rem(me + step, devices)
        return place(at // columns, lax.rem(at, columns))

    own = []
    for k in range(4):
        spot = wide_out[k].at[:, pl.ds(pl.multiple_of(me * wide_slots, wide_slots), wide_slots)]
        own.append(pltpu.make_async_copy(wide_in[k], spot, own_sem.at[k]))
        own[-1].start()

    barrier = pltpu.get_barrier_semaphore()

    @pl.loop(1, devices)
    def _(step):
        pl.semaphore_signal(barrier, inc=1, device_id=other(step), device_id_type=MESH)

    pl.semaphore_wait(barrier, devices - 1)

    def fine_copy(direction, k):
        up, across = DIRECTIONS[direction]
        target = place(brick + up, lax.rem(column + across + columns, columns))
        slot = 7 - direction
        return pltpu.make_async_remote_copy(
            src_ref=fine_in[k],
            dst_ref=fine_out[k].at[:, pl.ds(slot * slots, slots)],
            send_sem=fine_send.at[direction, k],
            recv_sem=fine_recv.at[slot, k],
            device_id=target,
            device_id_type=MESH,
        )

    def exists(direction):
        up = DIRECTIONS[direction][0]
        return jnp.logical_and(brick + up >= 0, brick + up < bricks)

    for direction in (0, 2, 5, 7, 1, 6, 3, 4):

        @pl.when(exists(direction))
        def _():
            for k in range(4):
                fine_copy(direction, k).start()

    def wide_copy(step, k):
        return pltpu.make_async_remote_copy(
            src_ref=wide_in[k],
            dst_ref=wide_out[k].at[:, pl.ds(pl.multiple_of(me * wide_slots, wide_slots), wide_slots)],
            send_sem=wide_send.at[step, k],
            recv_sem=wide_recv.at[step, k],
            device_id=other(step),
            device_id_type=MESH,
        )

    @pl.loop(1, devices)
    def _(step):
        for k in range(4):
            wide_copy(step, k).start()

    for direction in range(8):

        @pl.when(exists(direction))
        def _():
            for k in range(4):
                fine_copy(direction, k).wait_send()
                pltpu.make_async_copy(
                    fine_in[k],
                    fine_out[k].at[:, pl.ds(direction * slots, slots)],
                    fine_recv.at[direction, k],
                ).wait()

    @pl.loop(1, devices)
    def _(step):
        for k in range(4):
            wide_copy(step, k).wait()

    for k in range(4):
        own[k].wait()


def exchange(mesh_shape, fine, wide):
    bricks, reps, subs = (mesh_shape[name] for name in ("brick", "rep", "sub"))
    devices = bricks * reps * subs
    outs = [jax.ShapeDtypeStruct((a.shape[0], 8 * a.shape[1]), a.dtype) for a in fine]
    outs += [jax.ShapeDtypeStruct((a.shape[0], devices * a.shape[1]), a.dtype) for a in wide]
    vmem = pl.BlockSpec(memory_space=pltpu.VMEM)
    got = pl.pallas_call(
        functools.partial(exchange_kernel, bricks, reps, subs),
        out_shape=outs,
        in_specs=[vmem] * 8,
        out_specs=[vmem] * 8,
        scratch_shapes=[
            pltpu.SemaphoreType.DMA((8, 4)),
            pltpu.SemaphoreType.DMA((8, 4)),
            pltpu.SemaphoreType.DMA((devices, 4)),
            pltpu.SemaphoreType.DMA((devices, 4)),
            pltpu.SemaphoreType.DMA((4,)),
        ],
        compiler_params=pltpu.CompilerParams(collective_id=0, has_side_effects=True),
        name="exchange",
    )(*fine, *wide)
    return got[:4], got[4:]


def factor(cells, centre, radius, exponent, shift, period=None):
    gap = cells - centre
    if period is not None:
        half = period // 2
        gap = ((gap + half) & (period - 1)) - half
    spread = gap.astype(F32) - shift
    return jnp.where(jnp.abs(gap) <= radius, jnp.exp(-exponent * spread * spread), 0.0)


def stack_rows(cells, offset, exponent, charge):
    pad = jnp.zeros((6, exponent.shape[1]), F32)
    return jnp.concatenate([cells.astype(F32), offset, exponent, charge, pad], 0)


def halved(size, level):
    return lax.shift_right_logical(jnp.full(level.shape, size, I32), level)


def row_column_factors(table, rows, row_tile, row_block, columns, col_tile, col_block):
    whole = table[0:5].astype(I32)
    level, radius = whole[0:1], whole[1:2]
    exponent, charge = table[8:9], table[9:10]
    count = table.shape[1]
    row_cells = lax.broadcasted_iota(I32, (rows, count), 0)
    col_cells = lax.broadcasted_iota(I32, (columns, count), 0)
    row_centre = whole[2:3] - row_block * halved(row_tile, level)
    col_centre = whole[3:4] - col_block * halved(col_tile, level)
    row_weight = charge * factor(row_cells, row_centre, radius, exponent, table[5:6])
    col_factor = factor(
        col_cells, col_centre, radius, exponent, table[6:7], halved(GRID, level)
    )
    return level, row_weight, col_factor


def depth_factor(turned, width):
    whole = turned[:, 0:5].astype(I32)
    cells = lax.broadcasted_iota(I32, (turned.shape[0], width), 1)
    return factor(
        cells,
        whole[:, 4:5],
        whole[:, 1:2],
        turned[:, 8:9],
        turned[:, 7:8],
        halved(GRID, whole[:, 0:1]),
    ).astype(BF16)


def matmul(left, right):
    return jnp.dot(left, right, preferred_element_type=F32)


def collocate_kernel(bricks, columns_n, subs, steps, wide_block, *refs):
    fine, near, wide = refs[0:4], refs[4:8], refs[8:12]
    out0, out1, out2, out3, out4 = refs[12:17]
    depth, cols, row0, row1, spread_at, chunks = refs[17:]
    brick = lax.axis_index("brick")
    column = lax.axis_index("rep") * subs + lax.axis_index("sub")
    own_slots = fine[0].shape[1]
    outs = (out0, out1)
    row_tiles = [(ROWS >> level) // bricks for level in range(2)]
    col_tiles = [(GRID >> level) // columns_n for level in range(2)]
    periods = [GRID >> level for level in range(2)]
    rows = (row0, row1)

    def source(refs4, at, count):
        span = pl.ds(at, count)
        return stack_rows(refs4[0][:, span], refs4[3][:, span], refs4[1][:, span], refs4[2][:, span])

    def gather_spill(chunk):
        total = jnp.zeros((48, SPILL), F32)
        slots = lax.broadcasted_iota(I32, (SPILL, own_slots), 0).astype(F32) + (chunk * SPILL).astype(F32)
        for s in range(8):
            where_to = spread_at[s : s + 1, :]
            values = jnp.where(where_to >= 0, source(near, s * own_slots, own_slots), 0.0)
            high = values.astype(BF16)
            rest = values - high.astype(F32)
            middle = rest.astype(BF16)
            low = (rest - middle.astype(F32)).astype(BF16)
            pieces = jnp.concatenate([high, middle, low], 0)
            chosen = jnp.where(where_to == slots, 1.0, 0.0).astype(BF16)
            total += lax.dot_general(
                pieces, chosen, (((1,), (1,)), ((), ())), preferred_element_type=F32
            )
        return total[0:16] + total[16:32] + total[32:48]

    def fine_factors(table):
        level, row_weight, col_factor = row_column_factors(
            table, row_tiles[0], row_tiles[0], brick, col_tiles[0], col_tiles[0], column
        )
        first = jnp.where(level == 0, row_weight, 0.0)
        second = jnp.where(level == 1, row_weight[0 : row_tiles[1]], 0.0)
        return (first, second), col_factor, depth_factor(table.T, periods[0])

    def spill_places():
        def lined(k):
            return jnp.concatenate(
                [near[0][k : k + 1, s * own_slots : (s + 1) * own_slots] for s in range(8)], 0
            )

        level, radius, c0, c1 = (lined(k) for k in range(4))
        first = level == 0
        row_tile = jnp.where(first, row_tiles[0], row_tiles[1])
        col_tile = jnp.where(first, col_tiles[0], col_tiles[1])
        period = jnp.where(first, periods[0], periods[1])
        across = c0 - brick * row_tile
        along = ((c1 - column * col_tile + period // 2) & (period - 1)) - period // 2
        line = lax.broadcasted_iota(I32, level.shape, 0)
        up = jnp.where(line < 3, -1, jnp.where(line < 5, 0, 1)) + brick
        keep = (up >= 0) & (up < bricks)
        keep &= (across >= -radius) & (across < row_tile + radius)
        wrap = along + period
        keep &= ((along >= -radius) & (along < col_tile + radius)) | (wrap < col_tile + radius)
        keep = jnp.where(keep, 1.0, 0.0)
        count = own_slots // 128
        piled = jnp.concatenate([keep[:, i * 128 : (i + 1) * 128] for i in range(count)], 0)
        height = piled.shape[0]
        upper = lax.broadcasted_iota(I32, (128, 128), 0) <= lax.broadcasted_iota(I32, (128, 128), 1)
        within = matmul(piled.astype(BF16), jnp.where(upper, 1.0, 0.0).astype(BF16))
        sums = jnp.broadcast_to(within[:, 127:128], (height, 128))
        lower = lax.broadcasted_iota(I32, (height, height), 0) > lax.broadcasted_iota(
            I32, (height, height), 1
        )
        before = matmul(jnp.where(lower, 1.0, 0.0).astype(BF16), sums.astype(BF16))
        at = jnp.where(piled > 0.0, before + within - 1.0, -1.0)
        for i in range(count):
            spread_at[:, i * 128 : (i + 1) * 128] = at[i * 8 : (i + 1) * 8]
        chunks[0] = (jnp.max(at).astype(I32) + SPILL) // SPILL

    @pl.when(pl.program_id(0) == 0)
    def _():
        spill_places()
        table = jnp.concatenate([source(fine, 0, own_slots), gather_spill(jnp.int32(0))], 1)
        weights, cols[...], depth[...] = fine_factors(table)
        for level in range(2):
            rows[level][...] = weights[level]
        for ref in (out2, out3, out4):
            ref[...] = jnp.zeros(ref.shape, F32)

    step = pl.program_id(0)

    def wide_part(part):
        table = source(wide, pl.multiple_of(part * wide_block, wide_block), wide_block)
        share = (GRID >> 2) // bricks
        which, row_weight, col_factor = row_column_factors(
            table, ROWS >> 2, ROWS, 0, share, GRID // bricks, brick
        )
        depth_value = depth_factor(table.T, GRID >> 2)
        lanes = GRID >> 2
        for level, out in ((2, out2), (3, out3), (4, out4)):
            period = GRID >> level
            height = ROWS >> level
            share = period // bricks
            group = min(share, 8)
            copies = lanes // period
            width = min(copies, group)
            own = jnp.where(which == level, row_weight[0:height], 0.0)
            lane = lax.broadcasted_iota(I32, (height, lanes), 1) // period
            for first in range(0, share, group):
                weights = jnp.concatenate(
                    [(own * col_factor[i : i + 1]).astype(BF16) for i in range(first, first + group)], 0
                )
                result = matmul(weights, depth_value)
                for i in range(0, group, width):
                    piece = result[i * height : (i + 1) * height]
                    for j in range(1, width):
                        piece = jnp.where(lane == j, result[(i + j) * height : (i + j + 1) * height], piece)
                    start = (first + i) * period
                    out[:, start : start + width * period] += piece[:, 0 : width * period]

    def slab(level, row_ref, col_value, depth_value):
        per = row_tiles[level] // steps
        weights = jnp.concatenate(
            [(row_ref(step * per + i) * col_value).astype(BF16) for i in range(per)], 0
        )
        result = matmul(weights, depth_value)
        return result.reshape(per, col_tiles[level], periods[level])

    for level in range(2):
        outs[level][...] = slab(
            level,
            lambda r: rows[level][pl.ds(r, 1), :],
            cols[0 : col_tiles[level], :],
            depth[:, 0 : periods[level]],
        )

    parts = wide[0].shape[1] // wide_block // steps
    if parts == 1:
        wide_part(step)
    else:

        @pl.loop(0, parts)
        def _(part):
            wide_part(step * parts + part)

    def extra(chunk, carry):
        weights, col_factor, depth_value = fine_factors(gather_spill(chunk))
        for level in range(2):
            rows[level][:, 0:SPILL] = weights[level]
            outs[level][...] += slab(
                level,
                lambda r: rows[level][pl.ds(r, 1), 0:SPILL],
                col_factor[0 : col_tiles[level]],
                depth_value[:, 0 : periods[level]],
            )
        return carry

    @pl.when(chunks[0] > 1)
    def _():
        saved = [rows[level][:, 0:SPILL] for level in range(2)]
        lax.fori_loop(1, chunks[0], extra, 0)
        for level in range(2):
            rows[level][:, 0:SPILL] = saved[level]


def collocate(mesh_shape, fine, near, wide):
    bricks, reps, subs = (mesh_shape[name] for name in ("brick", "rep", "sub"))
    columns_n = reps * subs
    row_tiles = [(ROWS >> level) // bricks for level in range(2)]
    col_tiles = [(GRID >> level) // columns_n for level in range(2)]
    periods = [GRID >> level for level in range(2)]
    steps = min(8, row_tiles[1])
    count = fine[0].shape[1] + SPILL
    block = min(WIDE_BLOCK, wide[0].shape[1] // steps)

    def whole(shape):
        return pl.BlockSpec(shape, lambda i: (0,) * len(shape))

    shapes = [(row_tiles[level], col_tiles[level], periods[level]) for level in range(2)]
    shapes += [(ROWS >> level, (GRID >> level) ** 2 // bricks) for level in (2, 3, 4)]
    out_specs = [
        pl.BlockSpec((shape[0] // steps,) + shape[1:], lambda i: (i, 0, 0)) for shape in shapes[:2]
    ] + [whole(shape) for shape in shapes[2:]]
    scratch = [
        pltpu.VMEM((count, periods[0]), BF16),
        pltpu.VMEM((col_tiles[0], count), F32),
        pltpu.VMEM((row_tiles[0], count), F32),
        pltpu.VMEM((row_tiles[1], count), F32),
        pltpu.VMEM((8, fine[0].shape[1]), F32),
        pltpu.SMEM((1,), I32),
    ]
    operands = (*fine, *near, *wide)
    return pl.pallas_call(
        functools.partial(collocate_kernel, bricks, columns_n, subs, steps, block),
        grid=(steps,),
        out_shape=[jax.ShapeDtypeStruct(shape, F32) for shape in shapes],
        in_specs=[whole(a.shape) for a in operands],
        out_specs=out_specs,
        scratch_shapes=scratch,
        compiler_params=pltpu.CompilerParams(
            dimension_semantics=("arbitrary",), vmem_limit_bytes=56 * 1024 * 1024
        ),
        name="collocate",
    )(*operands)


def solution(mesh):
    shape = dict(mesh.shape)

    def per_device(
        fine_cells,
        fine_exponent,
        fine_charge,
        fine_offset,
        wide_cells,
        wide_exponent,
        wide_charge,
        wide_offset,
    ):
        fine = (fine_cells, fine_exponent[None, :], fine_charge[None, :], fine_offset)
        wide = (wide_cells, wide_exponent[None, :], wide_charge[None, :], wide_offset)
        near, wide_all = exchange(shape, fine, wide)
        return tuple(collocate(shape, fine, near, wide_all))

    split = P(("parts", "brick", "rep", "sub"))
    table = P(None, ("parts", "brick", "rep", "sub"))
    return jax.shard_map(
        per_device,
        mesh=mesh,
        in_specs=(table, split, split, table, table, split, split, table),
        out_specs=(
            P(("parts", "brick"), ("rep", "sub"), None),
            P(("parts", "brick"), ("rep", "sub"), None),
            P("parts", "brick"),
            P("parts", "brick"),
            P("parts", "brick"),
        ),
        check_vma=False,
    )
```

profile of v0, /device:TPU:0, one launch (start us, length us, event | category | flops | bytes accessed | tf_op | source)
XLA Modules:
  0.0 34.9 jit_solution(1224476904842821243)
XLA Ops:
  0.6 16.6 %exchange.1 = (s32[5,8192]{1,0:T(8,128)}, f32[1,8192]{1,0:T(1,128)}, f32[1,8192]{1,0:T(1,128)}, f32[3,8192]{1,0:T(4,128)}, s32[5,2048]{1,0:T(8,128)}, /*index=5*...) custom-call(s32[5,1024]{1,0:T(8,128)} %refs_0_.3, f32[1,1024]{1,0:T(1,128)} %bitcast.4, f32[1,1024]{1,0:T(1,128)} %bitcast.6, ...), custom_call_target="tpu_custom_call" | custom-call | tf_op jit(solution)/shard_map/exchange/pallas_call | solution.py:121
  17.2 17.7 %collocate.1 = (f32[32,128,512]{2,1,0:T(8,128)}, f32[16,64,256]{2,1,0:T(8,128)}, f32[32,4096]{1,0:T(8,128)}, f32[16,1024]{1,0:T(8,128)}, f32[8,256]{1,0:T(8,128)}) custom-call(s32[5,1024]{1,0:T(8,128)} %refs_0_.3, f32[1,1024]{1,0:T(1,128)} %bitcast.5, f32[1,1024]{1,0:T(1,128)} %bitcast.7, f32[3,1024]{1,0:T(4,128)} %refs_3_.3, ...), custom_call_target="tpu_custom_call" | custom-call | tf_op jit(solution)/shard_map/collocate/pallas_call | solution.py:380
where the time goes:
time: 35.1 us; the launch traced here: 34.9 us
  Pallas kernels  34.3 us (98%)
  between operations  0.64 us (2%)
    pallas_call x1, Pallas kernels, collocate(): pl.pallas_call(functools.partial(collocate_kernel, bricks, columns_n, sub...  17.7 us
    pallas_call x1, Pallas kernels, exchange(): pl.pallas_call(functools.partial(exchange_kernel, bricks, reps, subs), ou...  16.6 us

commit v1 on v0

v1 whole, which is shorter than its diff:
```python
import functools
import math

import jax
import jax.numpy as jnp
from jax import lax
from jax.experimental import pallas as pl
from jax.experimental.pallas import tpu as pltpu
from jax.sharding import PartitionSpec as P

GRID = 512
ROWS = 128
HALF = 4
SPILL = 384
WIDE_BLOCK = 1024
DIRECTIONS = [(i, j) for i in (-1, 0, 1) for j in (-1, 0, 1) if (i, j) != (0, 0)]
MESH = pl.DeviceIdType.MESH
F32 = jnp.float32
BF16 = jnp.bfloat16
I32 = jnp.int32
LOG2E = math.log2(math.e)
FLOATS = 5


def factor(cells, centre, radius, exponent, shift, period=None):
    reach = cells - (centre - radius)
    if period is not None:
        reach = reach & (period - 1)
        inside = reach <= 2 * radius
    else:
        inside = (reach >= 0) & (reach <= 2 * radius)
    spread = reach.astype(F32) - (radius.astype(F32) + shift)
    return jnp.where(inside, jnp.exp2((exponent * -LOG2E) * (spread * spread)), 0.0)


def halved(size, level):
    return lax.shift_right_logical(jnp.full(level.shape, size, I32), level)


def product(left, right):
    return lax.dot_general(left, right, (((1,), (1,)), ((), ())), preferred_element_type=F32)


def iota(shape):
    return lax.broadcasted_iota(I32, shape, 0)


def row_factor(cells, floats, rows, row_tile, row_block):
    level, radius = cells[0:1], cells[1:2]
    centre = cells[2:3] - row_block * halved(row_tile, level)
    shape = (rows, cells.shape[1])
    return floats[4:5] * factor(iota(shape), centre, radius, floats[3:4], floats[0:1])


def column_factor(cells, floats, columns, col_tile, col_block):
    level, radius = cells[0:1], cells[1:2]
    centre = cells[3:4] - col_block * halved(col_tile, level)
    shape = (columns, cells.shape[1])
    return factor(iota(shape), centre, radius, floats[3:4], floats[1:2], halved(GRID, level))


def depth_factor(cells, floats, width):
    level, radius = cells[0:1], cells[1:2]
    shape = (width, cells.shape[1])
    return factor(
        iota(shape), cells[4:5], radius, floats[3:4], floats[2:3], halved(GRID, level)
    ).astype(BF16)


def tiles(bricks, columns):
    row_tiles = [(ROWS >> level) // bricks for level in range(2)]
    col_tiles = [(GRID >> level) // columns for level in range(2)]
    periods = [GRID >> level for level in range(2)]
    return row_tiles, col_tiles, periods


def fine_factors(cells, floats, bricks, columns, brick, column):
    row_tiles, col_tiles, periods = tiles(bricks, columns)
    level = cells[0:1]
    row_weight = row_factor(cells, floats, row_tiles[0], row_tiles[0], brick)
    first = jnp.where(level == 0, row_weight, 0.0)
    second = jnp.where(level == 1, row_weight[0 : row_tiles[1]], 0.0)
    col = column_factor(cells, floats, col_tiles[0], col_tiles[0], column)
    return first, second, col, depth_factor(cells, floats, periods[0])


def local_kernel(bricks, reps, subs, *refs):
    fine_in, wide_in = refs[0:4], refs[4:8]
    near_i, near_f, wide_i, wide_f, part0, part1 = refs[8:14]
    own_i, own_f, own_wi, own_wf, depth, cols, row0, row1 = refs[14:22]
    fine_send, fine_recv, wide_send, wide_recv, own_sem, up_sem, down_sem = refs[22:]
    columns = reps * subs
    devices = bricks * columns
    brick = lax.axis_index("brick")
    column = lax.axis_index("rep") * subs + lax.axis_index("sub")
    me = brick * columns + column
    slots = own_i.shape[1]
    own_floats = own_f.at[:, 0:slots]
    wide_slots = wide_in[0].shape[1]
    row_tiles, col_tiles, periods = tiles(bricks, columns)
    parts = (part0, part1)
    rows = (row0, row1)

    def place(at_brick, at_column):
        return {"brick": at_brick, "rep": at_column // subs, "sub": at_column % subs}

    def at_column(step):
        return lax.rem(column + step, columns)

    def when_brick(step):
        return jnp.logical_and(brick + step >= 0, brick + step < bricks)

    barrier = pltpu.get_barrier_semaphore()

    def greet(step, first):
        @pl.when(when_brick(step))
        def _():
            @pl.loop(first, columns)
            def _(k):
                pl.semaphore_signal(
                    barrier, inc=1, device_id=place(brick + step, at_column(k)), device_id_type=MESH
                )

    greet(-1, 0)
    greet(0, 1)
    greet(1, 0)

    mine = pl.ds(pl.multiple_of(me * wide_slots, wide_slots), wide_slots)

    def fetches(source, whole_i, whole_f, first):
        pairs = [
            (source[0], whole_i),
            (source[3], whole_f.at[0:3]),
            (source[1], whole_f.at[3:4]),
            (source[2], whole_f.at[4:5]),
        ]
        return [
            pltpu.make_async_copy(a, b, own_sem.at[first + k]) for k, (a, b) in enumerate(pairs)
        ]

    own_wide = own_wf.at[:, 0:wide_slots]
    loads = fetches(wide_in, own_wi, own_wide, 0)
    loads += fetches(fine_in, own_i, own_floats, 4)
    for load in loads:
        load.start()
    for load in loads:
        load.wait()
    wide_i[:, mine] = own_wi[...]
    wide_f[:, mine] = own_wide[...]

    row0[...], row1[...], cols[...], depth[...] = fine_factors(
        own_i[...], own_floats[...], bricks, columns, brick, column
    )

    below = (brick > 0).astype(I32)
    above = (brick < bricks - 1).astype(I32)
    pl.semaphore_wait(barrier, columns - 1 + columns * (below + above))

    def wide_copy(to_brick, to_column, k):
        other = to_brick * columns + to_column
        return pltpu.make_async_remote_copy(
            src_ref=(own_wi, own_wide)[k],
            dst_ref=(wide_i, wide_f)[k].at[:, mine],
            send_sem=wide_send.at[other, k],
            recv_sem=wide_recv.at[me, k],
            device_id=place(to_brick, to_column),
            device_id_type=MESH,
        )

    def wide_to(to_brick, first):
        @pl.loop(first, columns)
        def _(step):
            for k in range(2):
                wide_copy(to_brick, at_column(step), k).start()

    def fine_copy(direction, k):
        up, across = DIRECTIONS[direction]
        slot = 7 - direction
        return pltpu.make_async_remote_copy(
            src_ref=(own_i, own_floats)[k],
            dst_ref=(near_i, near_f)[k].at[:, pl.ds(slot * slots, slots)],
            send_sem=fine_send.at[direction, k],
            recv_sem=fine_recv.at[slot, k],
            device_id=place(brick + up, at_column(across + columns)),
            device_id_type=MESH,
        )

    def token(step, sem):
        pl.semaphore_signal(sem, inc=1, device_id=place(brick + step, column), device_id_type=MESH)

    for step in (-1, 1):

        @pl.when(when_brick(step))
        def _():
            wide_to(brick + step, 0)

    wide_to(brick, 1)

    for direction in (1, 6, 0, 2, 5, 7, 3, 4):

        @pl.when(when_brick(DIRECTIONS[direction][0]))
        def _():
            for k in range(2):
                fine_copy(direction, k).start()

    @pl.when(brick >= 2)
    def _():
        pl.semaphore_wait(up_sem, 1)

    @pl.when(jnp.logical_and(brick >= 1, brick < bricks - 1))
    def _():
        token(1, up_sem)

    @pl.loop(0, jnp.maximum(brick - 1, 0))
    def _(to_brick):
        wide_to(to_brick, 0)

    def slab(level, first, per):
        weights = jnp.concatenate(
            [
                (rows[level][pl.ds(first + i, 1), :] * cols[0 : col_tiles[level], :]).astype(BF16)
                for i in range(per)
            ],
            0,
        )
        result = product(weights, depth[0 : periods[level], :])
        return result.reshape(per, col_tiles[level], periods[level])

    per1 = min(4, row_tiles[1])
    per0 = min(4, row_tiles[0])

    @pl.loop(0, row_tiles[1] // per1)
    def _(i):
        parts[1][pl.ds(i * per1, per1)] = slab(1, i * per1, per1)

    half0 = row_tiles[0] // per0 // 2

    @pl.loop(0, half0)
    def _(i):
        parts[0][pl.ds(i * per0, per0)] = slab(0, i * per0, per0)

    @pl.when(brick < bricks - 2)
    def _():
        pl.semaphore_wait(down_sem, 1)

    @pl.when(jnp.logical_and(brick >= 1, brick < bricks - 1))
    def _():
        token(-1, down_sem)

    @pl.loop(jnp.minimum(brick + 2, bricks), bricks)
    def _(to_brick):
        wide_to(to_brick, 0)

    @pl.loop(half0, row_tiles[0] // per0)
    def _(i):
        parts[0][pl.ds(i * per0, per0)] = slab(0, i * per0, per0)

    for direction in range(8):

        @pl.when(when_brick(DIRECTIONS[direction][0]))
        def _():
            for k in range(2):
                fine_copy(direction, k).wait_send()
                spot = (near_i, near_f)[k].at[:, pl.ds(direction * slots, slots)]
                own = (own_i, own_floats)[k]
                pltpu.make_async_copy(own, spot, fine_recv.at[direction, k]).wait()

    @pl.loop(1, devices)
    def _(step):
        at = lax.rem(me + step, devices)
        spot = pl.ds(pl.multiple_of(at * wide_slots, wide_slots), wide_slots)
        for k in range(2):
            wide_copy(at // columns, lax.rem(at, columns), k).wait_send()
            ref = (wide_i, wide_f)[k].at[:, spot]
            pltpu.make_async_copy((own_wi, own_wide)[k], ref, wide_recv.at[at, k]).wait()


def local_part(mesh_shape, fine, wide):
    bricks, reps, subs = (mesh_shape[name] for name in ("brick", "rep", "sub"))
    columns = reps * subs
    devices = bricks * columns
    row_tiles, col_tiles, periods = tiles(bricks, columns)
    slots, wide_slots = fine[0].shape[1], wide[0].shape[1]
    outs = [
        pltpu.VMEM((5, 8 * slots), I32),
        pltpu.VMEM((8, 8 * slots), F32),
        pltpu.VMEM((5, devices * wide_slots), I32),
        pltpu.VMEM((8, devices * wide_slots), F32),
    ] + [pltpu.VMEM((row_tiles[k], col_tiles[k], periods[k]), F32) for k in range(2)]
    return pl.pallas_call(
        functools.partial(local_kernel, bricks, reps, subs),
        out_shape=outs,
        in_specs=[pl.BlockSpec(memory_space=pltpu.HBM)] * 8,
        out_specs=[pl.BlockSpec(memory_space=pltpu.VMEM)] * 6,
        scratch_shapes=[
            pltpu.VMEM((5, slots), I32),
            pltpu.VMEM((8, slots + 128), F32),
            pltpu.VMEM((5, wide_slots), I32),
            pltpu.VMEM((8, wide_slots + 128), F32),
            pltpu.VMEM((periods[0], slots), BF16),
            pltpu.VMEM((col_tiles[0], slots), F32),
            pltpu.VMEM((row_tiles[0], slots), F32),
            pltpu.VMEM((row_tiles[1], slots), F32),
            pltpu.SemaphoreType.DMA((8, 2)),
            pltpu.SemaphoreType.DMA((8, 2)),
            pltpu.SemaphoreType.DMA((devices, 2)),
            pltpu.SemaphoreType.DMA((devices, 2)),
            pltpu.SemaphoreType.DMA((8,)),
            pltpu.SemaphoreType.REGULAR,
            pltpu.SemaphoreType.REGULAR,
        ],
        compiler_params=pltpu.CompilerParams(
            collective_id=0, has_side_effects=True, vmem_limit_bytes=30 * 1024 * 1024
        ),
        name="local_part",
    )(*[pltpu.with_memory_space_constraint(a, pltpu.HBM) for a in (*fine, *wide)])


def finish_kernel(bricks, columns, subs, slots, wide_block, *refs):
    near_i, near_f, wide_i, wide_f, part0, part1 = refs[0:6]
    out0, out1, out2, out3, out4 = refs[6:11]
    depth, cols, row0, row1, spread_at, chunks, sems = refs[11:]
    brick = lax.axis_index("brick")
    column = lax.axis_index("rep") * subs + lax.axis_index("sub")
    row_tiles, col_tiles, periods = tiles(bricks, columns)
    parts, outs, rows = (part0, part1), (out0, out1), (row0, row1)
    edge = 2 * HALF
    inner = [row_tiles[k] > 2 * HALF and col_tiles[k] > 2 * edge for k in range(2)]

    def copy_out(level, row, height, col, width, sem):
        spot = (pl.ds(row, height), pl.ds(col, width))
        return pltpu.make_async_copy(parts[level].at[spot], outs[level].at[spot], sems.at[sem])

    early, late = [], []
    for level in range(2):
        tall, wide_cols = row_tiles[level], col_tiles[level]
        base = 8 * level
        if inner[level]:
            height = tall - 2 * HALF
            early.append(copy_out(level, HALF, height, edge, wide_cols - 2 * edge, base))
            late.append(copy_out(level, HALF, height, 0, edge, base + 1))
            late.append(copy_out(level, HALF, height, wide_cols - edge, edge, base + 2))
            late.append(copy_out(level, 0, HALF, 0, wide_cols, base + 3))
            late.append(copy_out(level, tall - HALF, HALF, 0, wide_cols, base + 4))
        else:
            late.append(copy_out(level, 0, tall, 0, wide_cols, base + 1))
    for copy in early:
        copy.start()

    def gather_spill(chunk):
        ints = jnp.zeros((48, SPILL), F32)
        at = lax.broadcasted_iota(I32, (SPILL, slots), 0).astype(F32) + (chunk * SPILL).astype(F32)
        for s in range(8):
            where_to = spread_at[s : s + 1, :]
            span = pl.ds(s * slots, slots)
            pad = jnp.zeros((16 - 5 - FLOATS, slots), F32)
            table = jnp.concatenate([near_i[:, span].astype(F32), near_f[0:FLOATS, span], pad], 0)
            values = jnp.where(where_to >= 0, table, 0.0)
            high = values.astype(BF16)
            rest = values - high.astype(F32)
            middle = rest.astype(BF16)
            low = (rest - middle.astype(F32)).astype(BF16)
            pieces = jnp.concatenate([high, middle, low], 0)
            chosen = jnp.where(where_to == at, 1.0, 0.0).astype(BF16)
            ints += product(pieces, chosen)
        total = ints[0:16] + ints[16:32] + ints[32:48]
        return total[0:5].astype(I32), total[5 : 5 + FLOATS]

    def spill_places():
        def lined(k):
            return jnp.concatenate(
                [near_i[k : k + 1, s * slots : (s + 1) * slots] for s in range(8)], 0
            )

        level, radius, c0, c1 = (lined(k) for k in range(4))
        first = level == 0
        row_tile = jnp.where(first, row_tiles[0], row_tiles[1])
        col_tile = jnp.where(first, col_tiles[0], col_tiles[1])
        period = jnp.where(first, periods[0], periods[1])
        across = c0 - brick * row_tile
        along = ((c1 - column * col_tile + period // 2) & (period - 1)) - period // 2
        line = lax.broadcasted_iota(I32, level.shape, 0)
        up = jnp.where(line < 3, -1, jnp.where(line < 5, 0, 1)) + brick
        keep = (up >= 0) & (up < bricks)
        keep &= (across >= -radius) & (across < row_tile + radius)
        wrap = along + period
        keep &= ((along >= -radius) & (along < col_tile + radius)) | (wrap < col_tile + radius)
        keep = jnp.where(keep, 1.0, 0.0)
        count = slots // 128
        piled = jnp.concatenate([keep[:, i * 128 : (i + 1) * 128] for i in range(count)], 0)
        height = piled.shape[0]
        upper = lax.broadcasted_iota(I32, (128, 128), 0) <= lax.broadcasted_iota(I32, (128, 128), 1)
        within = jnp.dot(
            piled.astype(BF16), jnp.where(upper, 1.0, 0.0).astype(BF16), preferred_element_type=F32
        )
        sums = jnp.broadcast_to(within[:, 127:128], (height, 128))
        lower = lax.broadcasted_iota(I32, (height, height), 0) > lax.broadcasted_iota(
            I32, (height, height), 1
        )
        before = jnp.dot(
            jnp.where(lower, 1.0, 0.0).astype(BF16), sums.astype(BF16), preferred_element_type=F32
        )
        at = jnp.where(piled > 0.0, before + within - 1.0, -1.0)
        for i in range(count):
            spread_at[:, i * 128 : (i + 1) * 128] = at[i * 8 : (i + 1) * 8]
        chunks[0] = (jnp.max(at).astype(I32) + SPILL) // SPILL

    def add_rows(level, row, height, col, width):
        weights = jnp.concatenate(
            [
                (rows[level][row + i : row + i + 1, :] * cols[col : col + width, :]).astype(BF16)
                for i in range(height)
            ],
            0,
        )
        result = product(weights, depth[0 : periods[level], :])
        spot = (slice(row, row + height), slice(col, col + width))
        parts[level][spot] += result.reshape(height, width, periods[level])

    def add_spill(chunk):
        cells, floats = gather_spill(chunk)
        row0[...], row1[...], cols[...], depth[...] = fine_factors(
            cells, floats, bricks, columns, brick, column
        )
        for level in range(2):
            tall, wide_cols = row_tiles[level], col_tiles[level]
            if inner[level]:
                for row in (0, tall - HALF):
                    add_rows(level, row, HALF, 0, wide_cols)
                for row in range(HALF, tall - HALF, 8):
                    height = min(8, tall - HALF - row)
                    for col in (0, wide_cols - edge):
                        add_rows(level, row, height, col, edge)
            else:
                for row in range(0, tall, HALF):
                    add_rows(level, row, min(HALF, tall - row), 0, wide_cols)

    spill_places()
    add_spill(jnp.int32(0))

    @pl.loop(1, chunks[0])
    def _(chunk):
        add_spill(chunk)

    for copy in late:
        copy.start()

    def wide_part(part):
        span = pl.ds(pl.multiple_of(part * wide_block, wide_block), wide_block)
        cells, floats = wide_i[:, span], wide_f[0:FLOATS, span]
        share = (GRID >> 2) // bricks
        which = cells[0:1]
        row_weight = row_factor(cells, floats, ROWS >> 2, ROWS, 0)
        col = column_factor(cells, floats, share, GRID // bricks, brick)
        lanes = GRID >> 2
        depth_value = depth_factor(cells, floats, lanes)
        for level, out in ((2, out2), (3, out3), (4, out4)):
            period = GRID >> level
            height = ROWS >> level
            share = period // bricks
            group = min(share, 8)
            copies = lanes // period
            width = min(copies, group)
            own = jnp.where(which == level, row_weight[0:height], 0.0)
            lane = lax.broadcasted_iota(I32, (height, lanes), 1) // period
            for first in range(0, share, group):
                weights = jnp.concatenate(
                    [(own * col[i : i + 1]).astype(BF16) for i in range(first, first + group)], 0
                )
                result = product(weights, depth_value)
                for i in range(0, group, width):
                    piece = result[i * height : (i + 1) * height]
                    for j in range(1, width):
                        piece = jnp.where(
                            lane == j, result[(i + j) * height : (i + j + 1) * height], piece
                        )
                    start = (first + i) * period
                    out[:, start : start + width * period] += piece[:, 0 : width * period]

    for ref in (out2, out3, out4):
        ref[...] = jnp.zeros(ref.shape, F32)

    @pl.loop(0, wide_i.shape[1] // wide_block)
    def _(part):
        wide_part(part)

    for copy in early + late:
        copy.wait()


def finish(mesh_shape, slots, got):
    bricks, reps, subs = (mesh_shape[name] for name in ("brick", "rep", "sub"))
    columns = reps * subs
    row_tiles, col_tiles, periods = tiles(bricks, columns)
    block = min(WIDE_BLOCK, got[2].shape[1])
    shapes = [(row_tiles[level], col_tiles[level], periods[level]) for level in range(2)]
    shapes += [(ROWS >> level, (GRID >> level) ** 2 // bricks) for level in (2, 3, 4)]
    vmem, anywhere = pl.BlockSpec(memory_space=pltpu.VMEM), pl.BlockSpec(memory_space=pl.ANY)
    return pl.pallas_call(
        functools.partial(finish_kernel, bricks, columns, subs, slots, block),
        out_shape=[jax.ShapeDtypeStruct(shape, F32) for shape in shapes],
        in_specs=[vmem] * 6,
        out_specs=[anywhere] * 2 + [vmem] * 3,
        scratch_shapes=[
            pltpu.VMEM((periods[0], SPILL), BF16),
            pltpu.VMEM((col_tiles[0], SPILL), F32),
            pltpu.VMEM((row_tiles[0], SPILL), F32),
            pltpu.VMEM((row_tiles[1], SPILL), F32),
            pltpu.VMEM((8, slots), F32),
            pltpu.SMEM((1,), I32),
            pltpu.SemaphoreType.DMA((16,)),
        ],
        compiler_params=pltpu.CompilerParams(vmem_limit_bytes=30 * 1024 * 1024),
        name="finish",
    )(*got)


def solution(mesh):
    shape = dict(mesh.shape)

    def per_device(
        fine_cells,
        fine_exponent,
        fine_charge,
        fine_offset,
        wide_cells,
        wide_exponent,
        wide_charge,
        wide_offset,
    ):
        fine = (fine_cells, fine_exponent[None, :], fine_charge[None, :], fine_offset)
        wide = (wide_cells, wide_exponent[None, :], wide_charge[None, :], wide_offset)
        got = local_part(shape, fine, wide)
        return tuple(finish(shape, fine_cells.shape[1], got))

    split = P(("parts", "brick", "rep", "sub"))
    table = P(None, ("parts", "brick", "rep", "sub"))
    return jax.shard_map(
        per_device,
        mesh=mesh,
        in_specs=(table, split, split, table, table, split, split, table),
        out_specs=(
            P(("parts", "brick"), ("rep", "sub"), None),
            P(("parts", "brick"), ("rep", "sub"), None),
            P("parts", "brick"),
            P("parts", "brick"),
            P("parts", "brick"),
        ),
        check_vma=False,
    )
```

time: 35.1 us -> 25.7 us (0.73)
  Pallas kernels: 34.3 us -> 24.9 us
    pallas_call x2, Pallas kernels: 34.3 us -> 24.9 us  [the longest x1 16.5 us: local_part(): pl.pallas_call(functools.partial(local_kernel, bricks, reps, subs), out_s...]
where the time goes in v1:
time: 25.7 us; the launch traced here: 25.5 us
  Pallas kernels  24.9 us (97%)
  between operations  0.64 us (2%)
    pallas_call x1, Pallas kernels, local_part(): pl.pallas_call(functools.partial(local_kernel, bricks, reps, subs), out_s...  16.5 us
    pallas_call x1, Pallas kernels, finish(): pl.pallas_call(functools.partial(finish_kernel, bricks, columns, subs, sl...  8.37 us

profile of v1, /device:TPU:0, one launch (start us, length us, event | category | flops | bytes accessed | tf_op | source)
XLA Modules:
  0.0 25.5 jit_solution(15394670705006951867)
XLA Ops:
  0.6 16.5 %local_part.1 = (s32[5,8192]{1,0:T(8,128)S(1)}, f32[8,8192]{1,0:T(8,128)S(1)}, s32[5,2048]{1,0:T(8,128)S(1)}, f32[8,2048]{1,0:T(8,128)S(1)}, f32[32,128,512]{2,1,0:T(8,128)S(1)}, /*index=5*/f32[16,64,256]{2,1,0:T(8,128)S(1)}) custom-call(s32[5,1024]{1,0:T(8,128)} %refs_0_.1, f32[1,1024]{1,0:T(1,128)} %bitcast.4, f32[1,1024]{1,0:T(1,128)} %bitcast.5, ...), custom_call_target="tpu_custom_call" | custom-call | tf_op jit(solution)/shard_map/local_part/pallas_call | solution.py:290
  17.2 8.4 %finish.1 = (f32[32,128,512]{2,1,0:T(8,128)}, f32[16,64,256]{2,1,0:T(8,128)}, f32[32,4096]{1,0:T(8,128)}, f32[16,1024]{1,0:T(8,128)}, f32[8,256]{1,0:T(8,128)}) custom-call(s32[5,8192]{1,0:T(8,128)S(1)} %get-tuple-element.11.refs_0_, f32[8,8192]{1,0:T(8,128)S(1)} %get-tuple-element.12.refs_1_, s32[5,2048]{1,0:T(8,128)S(1)} %get-tuple-element.13.refs_2_, ...), custom_call_target="tpu_custom_call" | custom-call | tf_op jit(solution)/shard_map/finish/pallas_call | solution.py:499

commit v2 on v1

v2 whole, which is shorter than its diff:
```python
import functools
import math

import jax
import jax.numpy as jnp
from jax import lax
from jax.experimental import pallas as pl
from jax.experimental.pallas import tpu as pltpu
from jax.sharding import PartitionSpec as P

GRID = 512
ROWS = 128
HALF = 4
SPILL = 256
WIDE_BLOCK = 1024
DIRECTIONS = [(i, j) for i in (-1, 0, 1) for j in (-1, 0, 1) if (i, j) != (0, 0)]
MESH = pl.DeviceIdType.MESH
F32 = jnp.float32
BF16 = jnp.bfloat16
I32 = jnp.int32
LOG2E = math.log2(math.e)
FLOATS = 5
LISTS = 512
CAPS = (16, 160, 16, 48, 48, 16, 160, 16)
STARTS = (320, 160, 336, 384, 432, 352, 0, 368)
LANES = 128


def factor(cells, centre, radius, exponent, shift, period=None):
    reach = cells - (centre - radius)
    if period is not None:
        reach = reach & (period - 1)
        inside = reach <= 2 * radius
    else:
        inside = (reach >= 0) & (reach <= 2 * radius)
    spread = reach.astype(F32) - (radius.astype(F32) + shift)
    return jnp.where(inside, jnp.exp2((exponent * -LOG2E) * (spread * spread)), 0.0)


def halved(size, level):
    return lax.shift_right_logical(jnp.full(level.shape, size, I32), level)


def product(left, right):
    return lax.dot_general(left, right, (((1,), (1,)), ((), ())), preferred_element_type=F32)


def iota(shape):
    return lax.broadcasted_iota(I32, shape, 0)


def row_factor(cells, floats, rows, row_tile, row_block):
    level, radius = cells[0:1], cells[1:2]
    centre = cells[2:3] - row_block * halved(row_tile, level)
    shape = (rows, cells.shape[1])
    return floats[4:5] * factor(iota(shape), centre, radius, floats[3:4], floats[0:1])


def column_factor(cells, floats, columns, col_tile, col_block):
    level, radius = cells[0:1], cells[1:2]
    centre = cells[3:4] - col_block * halved(col_tile, level)
    shape = (columns, cells.shape[1])
    return factor(iota(shape), centre, radius, floats[3:4], floats[1:2], halved(GRID, level))


def depth_factor(cells, floats, width):
    level, radius = cells[0:1], cells[1:2]
    shape = (width, cells.shape[1])
    return factor(
        iota(shape), cells[4:5], radius, floats[3:4], floats[2:3], halved(GRID, level)
    ).astype(BF16)


def tiles(bricks, columns):
    row_tiles = [(ROWS >> level) // bricks for level in range(2)]
    col_tiles = [(GRID >> level) // columns for level in range(2)]
    periods = [GRID >> level for level in range(2)]
    return row_tiles, col_tiles, periods


def fine_factors(cells, floats, bricks, columns, brick, column):
    row_tiles, col_tiles, periods = tiles(bricks, columns)
    level = cells[0:1]
    row_weight = row_factor(cells, floats, row_tiles[0], row_tiles[0], brick)
    first = jnp.where(level == 0, row_weight, 0.0)
    second = jnp.where(level == 1, row_weight[0 : row_tiles[1]], 0.0)
    col = column_factor(cells, floats, col_tiles[0], col_tiles[0], column)
    return first, second, col, depth_factor(cells, floats, periods[0])


def ranks(keep, by_row):
    count = keep.shape[1] // LANES
    piled = jnp.concatenate([keep[:, i * LANES : (i + 1) * LANES] for i in range(count)], 0)
    height = piled.shape[0]
    square = (LANES, LANES)
    upper = iota(square) <= lax.broadcasted_iota(I32, square, 1)
    within = jnp.dot(
        piled.astype(BF16), jnp.where(upper, 1.0, 0.0).astype(BF16), preferred_element_type=F32
    )
    sums = jnp.broadcast_to(within[:, LANES - 1 : LANES], piled.shape)
    square = (height, height)
    gap = iota(square) - lax.broadcasted_iota(I32, square, 1)
    lower = gap > 0
    if by_row:
        lower &= (gap & 7) == 0
    before = jnp.dot(
        jnp.where(lower, 1.0, 0.0).astype(BF16), sums.astype(BF16), preferred_element_type=F32
    )
    at = before + within - 1.0
    return jnp.concatenate([at[i * 8 : (i + 1) * 8] for i in range(count)], 1)


def gather(cells, floats, chosen):
    count = cells.shape[1]
    pad = jnp.zeros((16 - 5 - FLOATS, count), F32)
    values = jnp.concatenate([cells.astype(F32), floats, pad], 0)
    high = values.astype(BF16)
    rest = values - high.astype(F32)
    middle = rest.astype(BF16)
    low = (rest - middle.astype(F32)).astype(BF16)
    found = product(jnp.concatenate([high, middle, low], 0), chosen)
    return found[0:16] + found[16:32] + found[32:48]


def by_line(values, shape):
    line = iota(shape)
    out = jnp.full(shape, values[0], F32)
    for k in range(1, len(values)):
        out = jnp.where(line == k, float(values[k]), out)
    return out


def touched(up, across, row_tile, col_tile, low0, high0, low1, high1):
    along0 = {-1: low0 < 0, 0: None, 1: high0 >= row_tile}[up]
    along1 = {-1: low1 < 0, 0: None, 1: high1 >= col_tile}[across]
    if along0 is None:
        return along1
    return along0 if along1 is None else along0 & along1


def add_spill(parts, rows, cols, depth, row_tiles, col_tiles, periods):
    edge = 2 * HALF

    def add_rows(level, row, height, col, width):
        weights = jnp.concatenate(
            [
                (rows[level][row + i : row + i + 1, :] * cols[col : col + width, :]).astype(BF16)
                for i in range(height)
            ],
            0,
        )
        result = product(weights, depth[0 : periods[level], :])
        spot = (slice(row, row + height), slice(col, col + width))
        parts[level][spot] += result.reshape(height, width, periods[level])

    for level in range(2):
        tall, wide = row_tiles[level], col_tiles[level]
        if tall > 2 * HALF and wide > 2 * edge:
            for row in (0, tall - HALF):
                add_rows(level, row, HALF, 0, wide)
            for col in (0, wide - edge):
                add_rows(level, HALF, tall - 2 * HALF, col, edge)
        else:
            for row in range(0, tall, HALF):
                add_rows(level, row, min(HALF, tall - row), 0, wide)


def local_kernel(bricks, reps, subs, *refs):
    fine_in, wide_in = refs[0:4], refs[4:8]
    wide_i, wide_f, part0, part1, over = refs[8:13]
    own_i, own_f, own_wi, own_wf, depth, cols, row0, row1 = refs[13:21]
    list_i, list_f, near_i, near_f, depth2, cols2, row02, row12 = refs[21:29]
    fine_send, fine_recv, wide_send, wide_recv, own_sem, up_sem, down_sem = refs[29:]
    columns = reps * subs
    devices = bricks * columns
    brick = lax.axis_index("brick")
    column = lax.axis_index("rep") * subs + lax.axis_index("sub")
    me = brick * columns + column
    slots = own_i.shape[1]
    own_floats = own_f.at[:, 0:slots]
    wide_slots = wide_in[0].shape[1]
    row_tiles, col_tiles, periods = tiles(bricks, columns)
    parts = (part0, part1)
    rows = (row0, row1)

    def place(at_brick, at_column):
        return {"brick": at_brick, "rep": at_column // subs, "sub": at_column % subs}

    def at_column(step):
        return lax.rem(column + step, columns)

    def when_brick(step):
        return jnp.logical_and(brick + step >= 0, brick + step < bricks)

    barrier = pltpu.get_barrier_semaphore()

    def greet(step, first):
        @pl.when(when_brick(step))
        def _():
            @pl.loop(first, columns)
            def _(k):
                pl.semaphore_signal(
                    barrier, inc=1, device_id=place(brick + step, at_column(k)), device_id_type=MESH
                )

    greet(-1, 0)
    greet(0, 1)
    greet(1, 0)

    mine = pl.ds(pl.multiple_of(me * wide_slots, wide_slots), wide_slots)

    def fetches(source, whole_i, whole_f, first):
        pairs = [
            (source[0], whole_i),
            (source[3], whole_f.at[0:3]),
            (source[1], whole_f.at[3:4]),
            (source[2], whole_f.at[4:5]),
        ]
        return [
            pltpu.make_async_copy(a, b, own_sem.at[first + k]) for k, (a, b) in enumerate(pairs)
        ]

    own_wide = own_wf.at[:, 0:wide_slots]
    loads = fetches(wide_in, own_wi.at[0:5, 0:wide_slots], own_wide, 0)
    loads += fetches(fine_in, own_i, own_floats, 4)
    for load in loads:
        load.start()
    for load in loads:
        load.wait()

    def lists():
        cells = own_i[...]
        level, radius = cells[0:1], cells[1:2]
        row_tile, col_tile = halved(row_tiles[0], level), halved(col_tiles[0], level)
        row, col = cells[2:3] - brick * row_tile, cells[3:4] - column * col_tile
        bounds = (row_tile, col_tile, row - radius, row + radius, col - radius, col + radius)
        keep = [
            jnp.where(touched(up, across, *bounds) & when_brick(up), 1.0, 0.0)
            for up, across in DIRECTIONS
        ]
        keep = jnp.concatenate(keep, 0)
        at = jnp.where(keep > 0.0, ranks(keep, True), -1.0)
        caps = by_line(CAPS, at.shape)
        lost = jnp.max(jnp.where(at >= caps, 1.0, 0.0))
        order = sorted(range(8), key=lambda d: STARTS[d])
        chosen = []
        for d in order:
            shape = (CAPS[d], slots)
            chosen.append(jnp.where(at[d : d + 1] == iota(shape).astype(F32), 1.0, 0.0))
        used = sum(CAPS)
        chosen.append(jnp.zeros((LISTS - used, slots), F32))
        found = gather(cells, own_floats[0:FLOATS, :], jnp.concatenate(chosen, 0).astype(BF16))
        list_i[...] = found[0:8].astype(I32)
        list_f[0:FLOATS] = found[5 : 5 + FLOATS]
        own_wi[5:8, 0:wide_slots] = jnp.broadcast_to(lost, (3, wide_slots)).astype(I32)

    lists()
    wide_i[:, mine] = own_wi[:, 0:wide_slots]
    wide_f[:, mine] = own_wide[...]

    below = (brick > 0).astype(I32)
    above = (brick < bricks - 1).astype(I32)
    pl.semaphore_wait(barrier, columns - 1 + columns * (below + above))

    def wide_copy(to_brick, to_column, k):
        other = to_brick * columns + to_column
        return pltpu.make_async_remote_copy(
            src_ref=(own_wi.at[:, 0:wide_slots], own_wide)[k],
            dst_ref=(wide_i, wide_f)[k].at[:, mine],
            send_sem=wide_send.at[other, k],
            recv_sem=wide_recv.at[me, k],
            device_id=place(to_brick, to_column),
            device_id_type=MESH,
        )

    def wide_to(to_brick, first):
        @pl.loop(first, columns)
        def _(step):
            for k in range(2):
                wide_copy(to_brick, at_column(step), k).start()

    def fine_copy(direction, k):
        up, across = DIRECTIONS[direction]
        slot = 7 - direction
        first, width = blocks(direction)
        return pltpu.make_async_remote_copy(
            src_ref=(list_i, list_f)[k].at[:, first : first + width],
            dst_ref=(near_i, near_f)[k].at[:, slot * 2 * LANES : slot * 2 * LANES + width],
            send_sem=fine_send.at[direction, k],
            recv_sem=fine_recv.at[slot, k],
            device_id=place(brick + up, at_column(across + columns)),
            device_id_type=MESH,
        )

    def token(step, sem):
        pl.semaphore_signal(sem, inc=1, device_id=place(brick + step, column), device_id_type=MESH)

    for step in (-1, 1):

        @pl.when(when_brick(step))
        def _():
            wide_to(brick + step, 0)

    wide_to(brick, 1)

    @pl.when(brick >= 2)
    def _():
        pl.semaphore_wait(up_sem, 1)

    @pl.when(jnp.logical_and(brick >= 1, brick < bricks - 1))
    def _():
        token(1, up_sem)

    @pl.when(jnp.logical_and(brick >= 1, brick == bricks - 2))
    def _():
        token(-1, down_sem)

    @pl.loop(0, jnp.maximum(brick - 1, 0))
    def _(to_brick):
        wide_to(to_brick, 0)

    for direction in (1, 6, 0, 2, 5, 7, 3, 4):

        @pl.when(when_brick(DIRECTIONS[direction][0]))
        def _():
            for k in range(2):
                fine_copy(direction, k).start()

    row0[...], row1[...], cols[...], depth[...] = fine_factors(
        own_i[...], own_floats[0:FLOATS, :], bricks, columns, brick, column
    )

    def slab(level, first, per):
        weights = jnp.concatenate(
            [
                (rows[level][pl.ds(first + i, 1), :] * cols[0 : col_tiles[level], :]).astype(BF16)
                for i in range(per)
            ],
            0,
        )
        result = product(weights, depth[0 : periods[level], :])
        return result.reshape(per, col_tiles[level], periods[level])

    per1 = min(16, row_tiles[1])
    per0 = min(16, row_tiles[0])

    @pl.loop(0, row_tiles[1] // per1)
    def _(i):
        parts[1][pl.ds(i * per1, per1)] = slab(1, i * per1, per1)

    def above_ready():
        @pl.when(brick < bricks - 2)
        def _():
            pl.semaphore_wait(down_sem, 1)

            @pl.when(brick >= 1)
            def _():
                token(-1, down_sem)

            @pl.loop(jnp.minimum(brick + 2, bricks), bricks)
            def _(to_brick):
                wide_to(to_brick, 0)

    @pl.when(brick >= 1)
    def _():
        above_ready()

    half0 = row_tiles[0] // per0 // 2

    @pl.loop(0, half0)
    def _(i):
        parts[0][pl.ds(i * per0, per0)] = slab(0, i * per0, per0)

    @pl.when(brick == 0)
    def _():
        above_ready()

    @pl.loop(half0, row_tiles[0] // per0)
    def _(i):
        parts[0][pl.ds(i * per0, per0)] = slab(0, i * per0, per0)

    for direction in range(8):

        @pl.when(when_brick(DIRECTIONS[direction][0]))
        def _():
            for k in range(2):
                fine_copy(direction, k).wait_send()
                fine_copy(7 - direction, k).wait_recv()

    def near_block(block):
        shape = (8, LANES)
        lane = lax.broadcasted_iota(I32, shape, 1) + block * LANES
        out_i, out_f = jnp.zeros(shape, I32), jnp.zeros(shape, F32)
        for d in range(8):
            first, width = blocks(d)
            if not first <= block * LANES < first + width:
                continue
            slot = 7 - d
            at = slot * 2 * LANES + block * LANES - first
            span = slice(at, at + LANES)
            valid = when_brick(-DIRECTIONS[d][0])
            inside = (lane >= STARTS[d]) & (lane < STARTS[d] + CAPS[d]) & valid
            out_i = jnp.where(inside, near_i[:, span], out_i)
            out_f = jnp.where(inside, near_f[:, span], out_f)
        return out_i, out_f

    pieces = [near_block(block) for block in range(LISTS // LANES)]
    row02[...], row12[...], cols2[...], depth2[...] = fine_factors(
        jnp.concatenate([a for a, b in pieces], 1),
        jnp.concatenate([b for a, b in pieces], 1),
        bricks,
        columns,
        brick,
        column,
    )
    add_spill(parts, (row02, row12), cols2, depth2, row_tiles, col_tiles, periods)

    @pl.loop(1, devices)
    def _(step):
        at = lax.rem(me + step, devices)
        spot = pl.ds(pl.multiple_of(at * wide_slots, wide_slots), wide_slots)
        for k in range(2):
            wide_copy(at // columns, lax.rem(at, columns), k).wait_send()
            ref = (wide_i, wide_f)[k].at[:, spot]
            own = (own_wi.at[:, 0:wide_slots], own_wide)[k]
            pltpu.make_async_copy(own, ref, wide_recv.at[at, k]).wait()

    over[0] = jnp.max(wide_i[5:6, :])


def blocks(direction):
    first = STARTS[direction] // LANES * LANES
    last = STARTS[direction] + CAPS[direction]
    return first, (last - first + LANES - 1) // LANES * LANES


def local_part(mesh_shape, fine, wide):
    bricks, reps, subs = (mesh_shape[name] for name in ("brick", "rep", "sub"))
    columns = reps * subs
    devices = bricks * columns
    row_tiles, col_tiles, periods = tiles(bricks, columns)
    slots, wide_slots = fine[0].shape[1], wide[0].shape[1]
    outs = [
        pltpu.VMEM((8, devices * wide_slots), I32),
        pltpu.VMEM((8, devices * wide_slots), F32),
    ] + [pltpu.VMEM((row_tiles[k], col_tiles[k], periods[k]), F32) for k in range(2)]
    outs += [jax.ShapeDtypeStruct((1,), I32)]
    return pl.pallas_call(
        functools.partial(local_kernel, bricks, reps, subs),
        out_shape=outs,
        in_specs=[pl.BlockSpec(memory_space=pltpu.HBM)] * 8,
        out_specs=[pl.BlockSpec(memory_space=pltpu.VMEM)] * 4
        + [pl.BlockSpec(memory_space=pltpu.SMEM)],
        scratch_shapes=[
            pltpu.VMEM((5, slots), I32),
            pltpu.VMEM((8, slots + 128), F32),
            pltpu.VMEM((8, wide_slots + 128), I32),
            pltpu.VMEM((8, wide_slots + 128), F32),
            pltpu.VMEM((periods[0], slots), BF16),
            pltpu.VMEM((col_tiles[0], slots), F32),
            pltpu.VMEM((row_tiles[0], slots), F32),
            pltpu.VMEM((row_tiles[1], slots), F32),
            pltpu.VMEM((8, LISTS), I32),
            pltpu.VMEM((8, LISTS), F32),
            pltpu.VMEM((8, 16 * LANES), I32),
            pltpu.VMEM((8, 16 * LANES), F32),
            pltpu.VMEM((periods[0], LISTS), BF16),
            pltpu.VMEM((col_tiles[0], LISTS), F32),
            pltpu.VMEM((row_tiles[0], LISTS), F32),
            pltpu.VMEM((row_tiles[1], LISTS), F32),
            pltpu.SemaphoreType.DMA((8, 2)),
            pltpu.SemaphoreType.DMA((8, 2)),
            pltpu.SemaphoreType.DMA((devices, 2)),
            pltpu.SemaphoreType.DMA((devices, 2)),
            pltpu.SemaphoreType.DMA((8,)),
            pltpu.SemaphoreType.REGULAR,
            pltpu.SemaphoreType.REGULAR,
        ],
        compiler_params=pltpu.CompilerParams(
            collective_id=0, has_side_effects=True, vmem_limit_bytes=30 * 1024 * 1024
        ),
        name="local_part",
    )(*[pltpu.with_memory_space_constraint(a, pltpu.HBM) for a in (*fine, *wide)])


def exchange_kernel(bricks, reps, subs, *refs):
    ins, outs = refs[0:4], refs[4:8]
    send, recv = refs[8:]
    columns = reps * subs
    brick = lax.axis_index("brick")
    column = lax.axis_index("rep") * subs + lax.axis_index("sub")
    slots = ins[0].shape[1]

    def place(direction):
        up, across = DIRECTIONS[direction]
        at = lax.rem(column + across + columns, columns)
        return {"brick": brick + up, "rep": at // subs, "sub": at % subs}

    def exists(direction):
        up = DIRECTIONS[direction][0]
        return jnp.logical_and(brick + up >= 0, brick + up < bricks)

    barrier = pltpu.get_barrier_semaphore()
    for direction in range(8):

        @pl.when(exists(direction))
        def _():
            pl.semaphore_signal(barrier, inc=1, device_id=place(direction), device_id_type=MESH)

    below = (brick > 0).astype(I32)
    above = (brick < bricks - 1).astype(I32)
    pl.semaphore_wait(barrier, 2 + 3 * (below + above))

    def copy(direction, k):
        slot = 7 - direction
        return pltpu.make_async_remote_copy(
            src_ref=ins[k],
            dst_ref=outs[k].at[:, pl.ds(slot * slots, slots)],
            send_sem=send.at[direction, k],
            recv_sem=recv.at[slot, k],
            device_id=place(direction),
            device_id_type=MESH,
        )

    for direction in range(8):

        @pl.when(exists(direction))
        def _():
            for k in range(4):
                copy(direction, k).start()

    for direction in range(8):

        @pl.when(exists(direction))
        def _():
            for k in range(4):
                copy(direction, k).wait_send()
                copy(7 - direction, k).wait_recv()


def exchange(mesh_shape, *fine):
    bricks, reps, subs = (mesh_shape[name] for name in ("brick", "rep", "sub"))
    vmem = pl.BlockSpec(memory_space=pltpu.VMEM)
    return pl.pallas_call(
        functools.partial(exchange_kernel, bricks, reps, subs),
        out_shape=[jax.ShapeDtypeStruct((a.shape[0], 8 * a.shape[1]), a.dtype) for a in fine],
        in_specs=[vmem] * 4,
        out_specs=[vmem] * 4,
        scratch_shapes=[pltpu.SemaphoreType.DMA((8, 4)), pltpu.SemaphoreType.DMA((8, 4))],
        compiler_params=pltpu.CompilerParams(
            collective_id=1, has_side_effects=True, vmem_limit_bytes=20 * 1024 * 1024
        ),
        name="exchange",
    )(*fine)


def repair_kernel(bricks, columns, subs, slots, *refs):
    near_i, exponent, charge, offset, grid0, grid1, out0, out1 = refs[0:8]
    part0, part1, depth, cols, row0, row1, spread_at, chunks, sems = refs[8:]
    brick = lax.axis_index("brick")
    column = lax.axis_index("rep") * subs + lax.axis_index("sub")
    row_tiles, col_tiles, periods = tiles(bricks, columns)
    parts, outs, rows = (part0, part1), (out0, out1), (row0, row1)
    loads = [pltpu.make_async_copy(outs[k], parts[k], sems.at[k]) for k in range(2)]
    for load in loads:
        load.start()
    for load in loads:
        load.wait()

    def near_table(span):
        return near_i[:, span], jnp.concatenate([offset[:, span], exponent[:, span], charge[:, span]], 0)

    def gather_spill(chunk):
        total = jnp.zeros((16, SPILL), F32)
        at = iota((SPILL, slots)).astype(F32) + (chunk * SPILL).astype(F32)
        for s in range(8):
            where_to = spread_at[s : s + 1, :]
            cells, floats = near_table(pl.ds(s * slots, slots))
            cells = jnp.where(where_to >= 0, cells, 0)
            floats = jnp.where(where_to >= 0, floats, 0.0)
            total += gather(cells, floats, jnp.where(where_to == at, 1.0, 0.0).astype(BF16))
        return total[0:8].astype(I32), total[5 : 5 + FLOATS]

    def spill_places():
        def lined(k):
            return jnp.concatenate(
                [near_i[k : k + 1, s * slots : (s + 1) * slots] for s in range(8)], 0
            )

        level, radius, c0, c1 = (lined(k) for k in range(4))
        first = level == 0
        row_tile = jnp.where(first, row_tiles[0], row_tiles[1])
        col_tile = jnp.where(first, col_tiles[0], col_tiles[1])
        keep = []
        for s in range(8):
            up, across = DIRECTIONS[7 - s]
            own = slice(s, s + 1)
            row = c0[own] - (brick - up) * row_tile[own]
            col = c1[own] - lax.rem(column - across + columns, columns) * col_tile[own]
            reach = radius[own]
            bounds = (row_tile[own], col_tile[own], row - reach, row + reach, col - reach, col + reach)
            valid = (brick - up >= 0) & (brick - up < bricks)
            keep.append(jnp.where(touched(up, across, *bounds) & valid, 1.0, 0.0))
        keep = jnp.concatenate(keep, 0)
        caps = by_line(CAPS[::-1], keep.shape)
        keep = jnp.where((keep > 0.0) & (ranks(keep, True) >= caps), 1.0, 0.0)
        at = jnp.where(keep > 0.0, ranks(keep, False), -1.0)
        spread_at[...] = at
        chunks[0] = (jnp.max(at).astype(I32) + SPILL) // SPILL

    spill_places()

    @pl.loop(0, chunks[0])
    def _(chunk):
        cells, floats = gather_spill(chunk)
        row0[...], row1[...], cols[...], depth[...] = fine_factors(
            cells, floats, bricks, columns, brick, column
        )
        add_spill(parts, rows, cols, depth, row_tiles, col_tiles, periods)

    copies = [pltpu.make_async_copy(parts[k], outs[k], sems.at[k]) for k in range(2)]
    for copy in copies:
        copy.start()
    for copy in copies:
        copy.wait()


def repair(mesh_shape, near, grids):
    bricks, reps, subs = (mesh_shape[name] for name in ("brick", "rep", "sub"))
    columns = reps * subs
    row_tiles, col_tiles, periods = tiles(bricks, columns)
    slots = near[0].shape[1] // 8
    vmem, anywhere = pl.BlockSpec(memory_space=pltpu.VMEM), pl.BlockSpec(memory_space=pltpu.HBM)
    return pl.pallas_call(
        functools.partial(repair_kernel, bricks, columns, subs, slots),
        out_shape=[pltpu.HBM(a.shape, a.dtype) for a in grids],
        in_specs=[vmem] * 4 + [anywhere] * 2,
        out_specs=[anywhere] * 2,
        input_output_aliases={4: 0, 5: 1},
        scratch_shapes=[pltpu.VMEM(a.shape, a.dtype) for a in grids]
        + [
            pltpu.VMEM((periods[0], SPILL), BF16),
            pltpu.VMEM((col_tiles[0], SPILL), F32),
            pltpu.VMEM((row_tiles[0], SPILL), F32),
            pltpu.VMEM((row_tiles[1], SPILL), F32),
            pltpu.VMEM((8, slots), F32),
            pltpu.SMEM((1,), I32),
            pltpu.SemaphoreType.DMA((2,)),
        ],
        compiler_params=pltpu.CompilerParams(vmem_limit_bytes=40 * 1024 * 1024),
        name="repair",
    )(*near, *grids)


def finish_kernel(bricks, wide_block, *refs):
    wide_i, wide_f, part0, part1 = refs[0:4]
    out0, out1, out2, out3, out4, sems = refs[4:]
    brick = lax.axis_index("brick")
    parts, outs = (part0, part1), (out0, out1)
    copies = [pltpu.make_async_copy(parts[k], outs[k], sems.at[k]) for k in range(2)]
    for copy in copies:
        copy.start()

    def wide_part(part):
        span = pl.ds(pl.multiple_of(part * wide_block, wide_block), wide_block)
        cells, floats = wide_i[:, span], wide_f[0:FLOATS, span]
        share = (GRID >> 2) // bricks
        which = cells[0:1]
        row_weight = row_factor(cells, floats, ROWS >> 2, ROWS, 0)
        col = column_factor(cells, floats, share, GRID // bricks, brick)
        lanes = GRID >> 2
        depth_value = depth_factor(cells, floats, lanes)
        for level, out in ((2, out2), (3, out3), (4, out4)):
            period = GRID >> level
            height = ROWS >> level
            share = period // bricks
            group = min(share, 8)
            copies = lanes // period
            width = min(copies, group)
            own = jnp.where(which == level, row_weight[0:height], 0.0)
            lane = lax.broadcasted_iota(I32, (height, lanes), 1) // period
            for first in range(0, share, group):
                weights = jnp.concatenate(
                    [(own * col[i : i + 1]).astype(BF16) for i in range(first, first + group)], 0
                )
                result = product(weights, depth_value)
                for i in range(0, group, width):
                    piece = result[i * height : (i + 1) * height]
                    for j in range(1, width):
                        piece = jnp.where(
                            lane == j, result[(i + j) * height : (i + j + 1) * height], piece
                        )
                    start = (first + i) * period
                    out[:, start : start + width * period] += piece[:, 0 : width * period]

    for ref in (out2, out3, out4):
        ref[...] = jnp.zeros(ref.shape, F32)

    @pl.loop(0, wide_i.shape[1] // wide_block)
    def _(part):
        wide_part(part)

    for copy in copies:
        copy.wait()


def finish(mesh_shape, got):
    bricks, reps, subs = (mesh_shape[name] for name in ("brick", "rep", "sub"))
    columns = reps * subs
    row_tiles, col_tiles, periods = tiles(bricks, columns)
    block = min(WIDE_BLOCK, got[0].shape[1])
    shapes = [(row_tiles[level], col_tiles[level], periods[level]) for level in range(2)]
    shapes += [(ROWS >> level, (GRID >> level) ** 2 // bricks) for level in (2, 3, 4)]
    vmem, anywhere = pl.BlockSpec(memory_space=pltpu.VMEM), pl.BlockSpec(memory_space=pltpu.HBM)
    return pl.pallas_call(
        functools.partial(finish_kernel, bricks, block),
        out_shape=[pltpu.HBM(shape, F32) for shape in shapes[:2]]
        + [jax.ShapeDtypeStruct(shape, F32) for shape in shapes[2:]],
        in_specs=[vmem] * 4,
        out_specs=[anywhere] * 2 + [vmem] * 3,
        scratch_shapes=[pltpu.SemaphoreType.DMA((2,))],
        compiler_params=pltpu.CompilerParams(vmem_limit_bytes=30 * 1024 * 1024),
        name="finish",
    )(*got[0:4])


def solution(mesh):
    shape = dict(mesh.shape)

    def per_device(
        fine_cells,
        fine_exponent,
        fine_charge,
        fine_offset,
        wide_cells,
        wide_exponent,
        wide_charge,
        wide_offset,
    ):
        fine = (fine_cells, fine_exponent[None, :], fine_charge[None, :], fine_offset)
        wide = (wide_cells, wide_exponent[None, :], wide_charge[None, :], wide_offset)
        got = local_part(shape, fine, wide)
        outs = finish(shape, got)

        def mend(state):
            near = exchange(shape, *fine)
            return (jnp.zeros((), I32), *repair(shape, near, state[1:]))

        state = lax.while_loop(lambda state: state[0] > 0, mend, (got[4][0], *outs[0:2]))
        return (*state[1:], *outs[2:])

    split = P(("parts", "brick", "rep", "sub"))
    table = P(None, ("parts", "brick", "rep", "sub"))
    return jax.shard_map(
        per_device,
        mesh=mesh,
        in_specs=(table, split, split, table, table, split, split, table),
        out_specs=(
            P(("parts", "brick"), ("rep", "sub"), None),
            P(("parts", "brick"), ("rep", "sub"), None),
            P("parts", "brick"),
            P("parts", "brick"),
            P("parts", "brick"),
        ),
        check_vma=False,
    )
```

time: 25.7 us -> 21.6 us (0.84)
  Pallas kernels: 24.9 us -> 19.7 us
  loops' own time: 0 us -> 0.81 us
    pallas_call x1, Pallas kernels: 8.37 us -> 4.57 us  [finish(): pl.pallas_call(functools.partial(finish_kernel, bricks, block), out_shape...]
    pallas_call x1, Pallas kernels: 16.5 us -> 15.1 us  [local_part(): pl.pallas_call(functools.partial(local_kernel, bricks, reps, subs), out_s...]
    another operation x0 -> x1, loops' own time: none -> 0.81 us  [per_device(): lax.while_loop(lambda state: state[0] > 0, mend, (got[4][0], *outs[0:2]))]
where the time goes in v2:
time: 21.6 us; the launch traced here: 21.4 us
  Pallas kernels  19.7 us (91%)
  between operations  0.87 us (4%)
  loops' own time  0.81 us (4%)
    pallas_call x1, Pallas kernels, local_part(): pl.pallas_call(functools.partial(local_kernel, bricks, reps, subs), out_s...  15.1 us
    pallas_call x1, Pallas kernels, finish(): pl.pallas_call(functools.partial(finish_kernel, bricks, block), out_shape...  4.57 us
    another operation x1, loops' own time, per_device(): lax.while_loop(lambda state: state[0] > 0, mend, (got[4][0], *outs[0:2]))  0.81 us

profile of v2, /device:TPU:0, one launch (start us, length us, event | category | flops | bytes accessed | tf_op | source)
XLA Modules:
  0.0 21.4 jit_solution(7629999866324750108)
XLA Ops:
  0.6 0.0 copy-start.2
  0.6 0.0 copy-start.3
  0.7 0.0 copy-start
  0.7 0.0 copy-start.1
  0.7 15.1 %local_part.1 = (s32[8,2048]{1,0:T(8,128)S(1)}, f32[8,2048]{1,0:T(8,128)S(1)}, f32[32,128,512]{2,1,0:T(8,128)S(1)}, f32[16,64,256]{2,1,0:T(8,128)S(1)}, s32[1]{0:T(128)}) custom-call(s32[5,1024]{1,0:T(8,128)} %refs_0_.1, f32[1,1024]{1,0:T(1,128)} %bitcast.5, f32[1,1024]{1,0:T(1,128)} %bitcast.7, f32[3,1024]{1,0:T(4,128)} %refs_3_.1, s32[5,128]{1,0:T(8,128)} %refs_4_.1, ...), custom_call_target="tpu_custom_call" | custom-call | tf_op jit(solution)/shard_map/local_part/pallas_call | solution.py:448
  15.8 4.6 %finish.1 = (f32[32,128,512]{2,1,0:T(8,128)}, f32[16,64,256]{2,1,0:T(8,128)}, f32[32,4096]{1,0:T(8,128)}, f32[16,1024]{1,0:T(8,128)}, f32[8,256]{1,0:T(8,128)}) custom-call(s32[8,2048]{1,0:T(8,128)S(1)} %get-tuple-element.59.refs_0_, f32[8,2048]{1,0:T(8,128)S(1)} %get-tuple-element.60.refs_1_, f32[32,128,512]{2,1,0:T(8,128)S(1)} %get-tuple-element.61.refs_2_, ...), custom_call_target="tpu_custom_call" | custom-call | tf_op jit(solution)/shard_map/finish/pallas_call | solution.py:715
  20.4 0.0 copy-done.2
  20.4 0.0 copy-done.3
  20.4 0.0 copy-done
  20.4 0.0 copy-done.1
  20.4 0.8 %while.11 = (s32[]{:T(128)}, f32[32,128,512]{2,1,0:T(8,128)}, f32[16,64,256]{2,1,0:T(8,128)}, s32[5,1024]{1,0:T(8,128)S(1)}, f32[1,1024]{1,0:T(1,128)S(1)}, /*index=5*/f32[1,1024]{1,0:T(1,128)S(1)}, f32[3,1024]{1,0:T(4,128)S(1)}) while((s32[]{:T(128)}, f32[32,128,512]{2,1,0:T(8,128)}, f32[16,64,256]{2,1,0:T(8,128)}, s32[5,1024]{1,0:T(8,128)S(1)}, ...), condition=%region_1.0_spmd, body=%region_0.0_spmd | while | flops 1 | bytes 73 | solution.py:749
Async XLA Ops:
  0.6 19.7 %copy-start.2 = (f32[1024]{0:T(1024)S(1)}, f32[1024]{0:T(1024)}, u32[]{:S(2)}) copy-start(f32[1024]{0:T(1024)} %param.11) | copy-start | bytes 12292
  0.6 19.7 %copy-start.3 = (f32[1024]{0:T(1024)S(1)}, f32[1024]{0:T(1024)}, u32[]{:S(2)}) copy-start(f32[1024]{0:T(1024)} %param.12) | copy-start | bytes 12292
  0.7 19.7 %copy-start = (s32[5,1024]{1,0:T(8,128)S(1)}, s32[5,1024]{1,0:T(8,128)}, u32[]{:S(2)}) copy-start(s32[5,1024]{1,0:T(8,128)} %refs_0_.1) | copy-start | bytes 61444
  0.7 19.7 %copy-start.1 = (f32[3,1024]{1,0:T(4,128)S(1)}, f32[3,1024]{1,0:T(4,128)}, u32[]{:S(2)}) copy-start(f32[3,1024]{1,0:T(4,128)} %refs_3_.1) | copy-start | bytes 36868

commit v3 on v2

--- a/solution.py
+++ b/solution.py
@@ -170,7 +170,7 @@
     wide_i, wide_f, part0, part1, over = refs[8:13]
     own_i, own_f, own_wi, own_wf, depth, cols, row0, row1 = refs[13:21]
     list_i, list_f, near_i, near_f, depth2, cols2, row02, row12 = refs[21:29]
-    fine_send, fine_recv, wide_send, wide_recv, own_sem, up_sem, down_sem = refs[29:]
+    fine_send, fine_recv, wide_send, wide_recv, own_sem = refs[29:]
     columns = reps * subs
     devices = bricks * columns
     brick = lax.axis_index("brick")
@@ -183,29 +183,34 @@
     parts = (part0, part1)
     rows = (row0, row1)
 
-    def place(at_brick, at_column):
-        return {"brick": at_brick, "rep": at_column // subs, "sub": at_column % subs}
-
-    def at_column(step):
-        return lax.rem(column + step, columns)
+    rep_at, sub_at = lax.axis_index("rep"), lax.axis_index("sub")
+    sides = {0: (rep_at, sub_at)}
+    for across in (-1, 1):
+        at = lax.rem(column + across + columns, columns)
+        sides[across] = (lax.div(at, subs), lax.rem(at, subs))
+
+    def place(at_brick, at_rep, at_sub):
+        return {"brick": at_brick, "rep": at_rep, "sub": at_sub}
+
+    def each_column(at_brick, act):
+        for k in range(columns):
+
+            @pl.when(at_brick * columns + k != me)
+            def _():
+                act(at_brick, k)
 
     def when_brick(step):
         return jnp.logical_and(brick + step >= 0, brick + step < bricks)
 
     barrier = pltpu.get_barrier_semaphore()
 
-    def greet(step, first):
-        @pl.when(when_brick(step))
-        def _():
-            @pl.loop(first, columns)
-            def _(k):
-                pl.semaphore_signal(
-                    barrier, inc=1, device_id=place(brick + step, at_column(k)), device_id_type=MESH
-                )
-
-    greet(-1, 0)
-    greet(0, 1)
-    greet(1, 0)
+    def greet(at_brick, k):
+        where = place(at_brick, k // subs, k % subs)
+        pl.semaphore_signal(barrier, inc=1, device_id=where, device_id_type=MESH)
+
+    @pl.loop(0, bricks)
+    def _(at_brick):
+        each_column(at_brick, greet)
 
     mine = pl.ds(pl.multiple_of(me * wide_slots, wide_slots), wide_slots)
 
@@ -258,10 +263,6 @@
     wide_i[:, mine] = own_wi[:, 0:wide_slots]
     wide_f[:, mine] = own_wide[...]
 
-    below = (brick > 0).astype(I32)
-    above = (brick < bricks - 1).astype(I32)
-    pl.semaphore_wait(barrier, columns - 1 + columns * (below + above))
-
     def wide_copy(to_brick, to_column, k):
         other = to_brick * columns + to_column
         return pltpu.make_async_remote_copy(
@@ -269,15 +270,16 @@
             dst_ref=(wide_i, wide_f)[k].at[:, mine],
             send_sem=wide_send.at[other, k],
             recv_sem=wide_recv.at[me, k],
-            device_id=place(to_brick, to_column),
+            device_id=place(to_brick, to_column // subs, to_column % subs),
             device_id_type=MESH,
         )
 
-    def wide_to(to_brick, first):
-        @pl.loop(first, columns)
-        def _(step):
+    def wide_to(to_brick):
+        def start(at_brick, column_at):
             for k in range(2):
-                wide_copy(to_brick, at_column(step), k).start()
+                wide_copy(at_brick, column_at, k).start()
+
+        each_column(to_brick, start)
 
     def fine_copy(direction, k):
         up, across = DIRECTIONS[direction]
@@ -288,47 +290,9 @@
             dst_ref=(near_i, near_f)[k].at[:, slot * 2 * LANES : slot * 2 * LANES + width],
             send_sem=fine_send.at[direction, k],
             recv_sem=fine_recv.at[slot, k],
-            device_id=place(brick + up, at_column(across + columns)),
+            device_id=place(brick + up, *sides[across]),
             device_id_type=MESH,
         )
-
-    def token(step, sem):
-        pl.semaphore_signal(sem, inc=1, device_id=place(brick + step, column), device_id_type=MESH)
-
-    for step in (-1, 1):
-
-        @pl.when(when_brick(step))
-        def _():
-            wide_to(brick + step, 0)
-
-    wide_to(brick, 1)
-
-    @pl.when(brick >= 2)
-    def _():
-        pl.semaphore_wait(up_sem, 1)
-
-    @pl.when(jnp.logical_and(brick >= 1, brick < bricks - 1))
-    def _():
-        token(1, up_sem)
-
-    @pl.when(jnp.logical_and(brick >= 1, brick == bricks - 2))
-    def _():
-        token(-1, down_sem)
-
-    @pl.loop(0, jnp.maximum(brick - 1, 0))
-    def _(to_brick):
-        wide_to(to_brick, 0)
-
-    for direction in (1, 6, 0, 2, 5, 7, 3, 4):
-
-        @pl.when(when_brick(DIRECTIONS[direction][0]))
-        def _():
-            for k in range(2):
-                fine_copy(direction, k).start()
-
-    row0[...], row1[...], cols[...], depth[...] = fine_factors(
-        own_i[...], own_floats[0:FLOATS, :], bricks, columns, brick, column
-    )
 
     def slab(level, first, per):
         weights = jnp.concatenate(
@@ -339,45 +303,52 @@
             0,
         )
         result = product(weights, depth[0 : periods[level], :])
-        return result.reshape(per, col_tiles[level], periods[level])
+        parts[level][pl.ds(first, per)] = result.reshape(per, col_tiles[level], periods[level])
+
+    def send():
+        pl.semaphore_wait(barrier, devices - 1)
+
+        @pl.loop(0, brick)
+        def _(to_brick):
+            wide_to(to_brick)
+
+        for direction in (1, 6, 0, 2, 5, 7, 3, 4):
+
+            @pl.when(when_brick(DIRECTIONS[direction][0]))
+            def _():
+                for k in range(2):
+                    fine_copy(direction, k).start()
+
+        wide_to(brick)
+
+        @pl.loop(brick + 1, bricks)
+        def _(to_brick):
+            wide_to(to_brick)
 
     per1 = min(16, row_tiles[1])
     per0 = min(16, row_tiles[0])
-
-    @pl.loop(0, row_tiles[1] // per1)
-    def _(i):
-        parts[1][pl.ds(i * per1, per1)] = slab(1, i * per1, per1)
-
-    def above_ready():
-        @pl.when(brick < bricks - 2)
+    halves = row_tiles[0] // per0
+    gate = jnp.minimum((bricks - brick) // 2, halves + 1)
+
+    @pl.loop(0, halves + 2)
+    def _(stage):
+        @pl.when(stage == gate)
         def _():
-            pl.semaphore_wait(down_sem, 1)
-
-            @pl.when(brick >= 1)
+            send()
+
+        @pl.when(stage == 0)
+        def _():
+            row0[...], row1[...], cols[...], depth[...] = fine_factors(
+                own_i[...], own_floats[0:FLOATS, :], bricks, columns, brick, column
+            )
+            for i in range(row_tiles[1] // per1):
+                slab(1, i * per1, per1)
+
+        for half in range(halves):
+
+            @pl.when(stage == half + 1)
             def _():
-                token(-1, down_sem)
-
-            @pl.loop(jnp.minimum(brick + 2, bricks), bricks)
-            def _(to_brick):
-                wide_to(to_brick, 0)
-
-    @pl.when(brick >= 1)
-    def _():
-        above_ready()
-
-    half0 = row_tiles[0] // per0 // 2
-
-    @pl.loop(0, half0)
-    def _(i):
-        parts[0][pl.ds(i * per0, per0)] = slab(0, i * per0, per0)
-
-    @pl.when(brick == 0)
-    def _():
-        above_ready()
-
-    @pl.loop(half0, row_tiles[0] // per0)
-    def _(i):
-        parts[0][pl.ds(i * per0, per0)] = slab(0, i * per0, per0)
+                slab(0, half * per0, per0)
 
     for direction in range(8):
 
@@ -415,15 +386,18 @@
     )
     add_spill(parts, (row02, row12), cols2, depth2, row_tiles, col_tiles, periods)
 
-    @pl.loop(1, devices)
-    def _(step):
-        at = lax.rem(me + step, devices)
+    def arrive(at_brick, column_at):
+        at = at_brick * columns + column_at
         spot = pl.ds(pl.multiple_of(at * wide_slots, wide_slots), wide_slots)
         for k in range(2):
-            wide_copy(at // columns, lax.rem(at, columns), k).wait_send()
+            wide_copy(at_brick, column_at, k).wait_send()
             ref = (wide_i, wide_f)[k].at[:, spot]
             own = (own_wi.at[:, 0:wide_slots], own_wide)[k]
             pltpu.make_async_copy(own, ref, wide_recv.at[at, k]).wait()
+
+    @pl.loop(0, bricks)
+    def _(at_brick):
+        each_column(at_brick, arrive)
 
     over[0] = jnp.max(wide_i[5:6, :])
 
@@ -473,8 +447,6 @@
             pltpu.SemaphoreType.DMA((devices, 2)),
             pltpu.SemaphoreType.DMA((devices, 2)),
             pltpu.SemaphoreType.DMA((8,)),
-            pltpu.SemaphoreType.REGULAR,
-            pltpu.SemaphoreType.REGULAR,
         ],
         compiler_params=pltpu.CompilerParams(
             collective_id=0, has_side_effects=True, vmem_limit_bytes=30 * 1024 * 1024

time: 21.6 us -> 20.2 us (0.935)
  Pallas kernels: 19.7 us -> 18.3 us
    pallas_call x1, Pallas kernels: 15.1 us -> 13.7 us  [local_part(): pl.pallas_call(functools.partial(local_kernel, bricks, reps, subs), out_s...]
where the time goes in v3:
time: 20.2 us; the launch traced here: 20 us
  Pallas kernels  18.3 us (91%)
  between operations  0.87 us (4%)
  loops' own time  0.81 us (4%)
    pallas_call x1, Pallas kernels, local_part(): pl.pallas_call(functools.partial(local_kernel, bricks, reps, subs), out_s...  13.7 us
    pallas_call x1, Pallas kernels, finish(): pl.pallas_call(functools.partial(finish_kernel, bricks, block), out_shape...  4.57 us
    another operation x1, loops' own time, per_device(): lax.while_loop(lambda state: state[0] > 0, mend, (got[4][0], *outs[0:2]))  0.81 us

profile of v3, /device:TPU:0, one launch (start us, length us, event | category | flops | bytes accessed | tf_op | source)
XLA Modules:
  0.0 20.0 jit_solution(8366677104259459893)
XLA Ops:
  0.6 0.0 copy-start.2
  0.6 0.0 copy-start.3
  0.7 0.0 copy-start
  0.7 0.0 copy-start.1
  0.7 13.7 %local_part.1 = (s32[8,2048]{1,0:T(8,128)S(1)}, f32[8,2048]{1,0:T(8,128)S(1)}, f32[32,128,512]{2,1,0:T(8,128)S(1)}, f32[16,64,256]{2,1,0:T(8,128)S(1)}, s32[1]{0:T(128)}) custom-call(s32[5,1024]{1,0:T(8,128)} %refs_0_.1, f32[1,1024]{1,0:T(1,128)} %bitcast.5, f32[1,1024]{1,0:T(1,128)} %bitcast.7, f32[3,1024]{1,0:T(4,128)} %refs_3_.1, s32[5,128]{1,0:T(8,128)} %refs_4_.1, ...), custom_call_target="tpu_custom_call" | custom-call | tf_op jit(solution)/shard_map/local_part/pallas_call | solution.py:422
  14.4 4.6 %finish.1 = (f32[32,128,512]{2,1,0:T(8,128)}, f32[16,64,256]{2,1,0:T(8,128)}, f32[32,4096]{1,0:T(8,128)}, f32[16,1024]{1,0:T(8,128)}, f32[8,256]{1,0:T(8,128)}) custom-call(s32[8,2048]{1,0:T(8,128)S(1)} %get-tuple-element.59.refs_0_, f32[8,2048]{1,0:T(8,128)S(1)} %get-tuple-element.60.refs_1_, f32[32,128,512]{2,1,0:T(8,128)S(1)} %get-tuple-element.61.refs_2_, ...), custom_call_target="tpu_custom_call" | custom-call | tf_op jit(solution)/shard_map/finish/pallas_call | solution.py:687
  19.0 0.0 copy-done.2
  19.0 0.0 copy-done.3
  19.0 0.0 copy-done
  19.0 0.0 copy-done.1
  19.0 0.8 %while.11 = (s32[]{:T(128)}, f32[32,128,512]{2,1,0:T(8,128)}, f32[16,64,256]{2,1,0:T(8,128)}, s32[5,1024]{1,0:T(8,128)S(1)}, f32[1,1024]{1,0:T(1,128)S(1)}, /*index=5*/f32[1,1024]{1,0:T(1,128)S(1)}, f32[3,1024]{1,0:T(4,128)S(1)}) while((s32[]{:T(128)}, f32[32,128,512]{2,1,0:T(8,128)}, f32[16,64,256]{2,1,0:T(8,128)}, s32[5,1024]{1,0:T(8,128)S(1)}, ...), condition=%region_1.0_spmd, body=%region_0.0_spmd | while | flops 1 | bytes 73 | solution.py:721
Async XLA Ops:
  0.6 18.4 %copy-start.2 = (f32[1024]{0:T(1024)S(1)}, f32[1024]{0:T(1024)}, u32[]{:S(2)}) copy-start(f32[1024]{0:T(1024)} %param.11) | copy-start | bytes 12292
  0.6 18.4 %copy-start.3 = (f32[1024]{0:T(1024)S(1)}, f32[1024]{0:T(1024)}, u32[]{:S(2)}) copy-start(f32[1024]{0:T(1024)} %param.12) | copy-start | bytes 12292
  0.7 18.4 %copy-start = (s32[5,1024]{1,0:T(8,128)S(1)}, s32[5,1024]{1,0:T(8,128)}, u32[]{:S(2)}) copy-start(s32[5,1024]{1,0:T(8,128)} %refs_0_.1) | copy-start | bytes 61444
  0.7 18.4 %copy-start.1 = (f32[3,1024]{1,0:T(4,128)S(1)}, f32[3,1024]{1,0:T(4,128)}, u32[]{:S(2)}) copy-start(f32[3,1024]{1,0:T(4,128)} %refs_3_.1) | copy-start | bytes 36868
